TPU v7x, 32 devices: a whole 2x2x4 slice. The times are simulated.
32 devices in a mesh: expert: 8 (over y, x, core), dp: 4 (over z).
Axes of the slice: x: 2, y: 2, z: 4, core: 2. Of those that a mesh axis runs over, the one named last changes fastest.
Arguments:
- gradient: bfloat16 [4, 1, 14336, 2048], P('dp', None, None, 'expert'), may hold values from -6 to 6
- momentum: float32 [4, 1, 14336, 2048], P('dp', None, 'expert'), may hold values from -6 to 6
- group_index: int32 [224, 32, 4, 32], P('expert'), may hold values from 0 to 4095, all different within a row
Outputs:
- momentum_next: float32 [4, 1, 14336, 2048], P('dp', None, 'expert')
- update: float32 [1, 14336, 2048], P(None, None, 'expert')
Inputs may be any that keep to these rules, and one draw needn't show every extreme that they name: `group_index`: an entry names the coefficient at row frequency (entry // 64) and column frequency (entry % 64) of its block; the 32 entries of one block and replica differ.
All inputs are finite; a program needn't handle non-finite values.
Results may differ from a plain program's by a relative error of at most 0.0003.
Values may be sent and summed in bfloat16 or wider, within the bound.
No kernel may reach another device: no remote copies, remote signals or barrier semaphores. Data moves between devices by JAX's collectives and lax.ppermute only.
A program may use at most 192 MiB of HBM per device.

v0:
```python
import math
import jax
import jax.numpy as jnp
from jax import lax
from jax.sharding import PartitionSpec as P

SPAN = 64
MOMENTUM_DECAY = 0.999
HIGHEST_PRECISION = lax.Precision.HIGHEST


def cosine_table(order_size):
    frequency = jnp.arange(order_size, dtype=jnp.float32)[:, None]
    position = jnp.arange(order_size, dtype=jnp.float32)[None, :]
    weighting = jnp.where(frequency == 0, math.sqrt(1.0 / order_size), math.sqrt(2.0 / order_size))
    return weighting * jnp.cos(math.pi * (2.0 * position + 1.0) * frequency / (2.0 * order_size))


def forward(blocks, cosine):
    return jnp.einsum("ui,piqj,vj->pquv", cosine, blocks, cosine, precision=HIGHEST_PRECISION)


def inverse(coeffs, cosine):
    return jnp.einsum("ui,pquv,vj->piqj", cosine, coeffs, cosine, precision=HIGHEST_PRECISION)


def place(values, picked, total):
    count_rows = picked.shape[0]
    count_cols = picked.shape[1]
    row_ids = jnp.arange(count_rows, dtype=jnp.int32)[:, None, None]
    col_ids = jnp.arange(count_cols, dtype=jnp.int32)[None, :, None]
    empty = jnp.zeros((count_rows, count_cols, total), jnp.float32)
    return empty.at[row_ids, col_ids, picked].add(values)


def on_device(gradient, momentum, group_index):
    cosine = cosine_table(SPAN)
    replica = lax.axis_index("dp")
    shifted = lax.all_to_all(gradient, "expert", split_axis=2, concat_axis=3, tiled=True)
    row_count = shifted.shape[1] * shifted.shape[2]
    col_count = shifted.shape[3]
    decayed = MOMENTUM_DECAY * momentum.reshape(row_count, col_count) + shifted.reshape(
        row_count, col_count
    ).astype(jnp.float32)
    block_rows = row_count // SPAN
    block_cols = col_count // SPAN
    blocks = decayed.reshape(block_rows, SPAN, block_cols, SPAN)
    coeffs = forward(blocks, cosine).reshape(block_rows, block_cols, SPAN * SPAN)
    own = lax.dynamic_index_in_dim(group_index, replica, 2, keepdims=False)
    values = jnp.take_along_axis(coeffs, own, axis=2)
    selected = place(values, own, SPAN * SPAN).reshape(block_rows, block_cols, SPAN, SPAN)
    restored = inverse(selected, cosine).reshape(row_count, col_count)
    momentum_next = (decayed - restored).reshape(momentum.shape)
    total = lax.psum(restored, "dp")
    update = lax.all_to_all(total[None], "expert", split_axis=2, concat_axis=1, tiled=True)
    return (momentum_next, update)


def solution(mesh):
    placed = (
        P("dp", None, None, "expert"),
        P("dp", None, "expert", None),
        P("expert", None, None, None),
    )
    return jax.shard_map(
        on_device,
        mesh=mesh,
        in_specs=placed,
        out_specs=(P("dp", None, "expert", None), P(None, None, "expert")),
        check_vma=False,
    )
```

profile of v0, /device:TPU:0, one launch (start us, length us, event | category | flops | bytes accessed | tf_op | source)
XLA Modules:
  0.0 1791.6 jit_solution(7726705985942069426)
XLA Ops:
  7.2 13.9 copy.47
  21.6 74.4 %reduce.4 = bf16[14336,256]{1,0:T(8,128)(2,1)} reduce(bf16[14336,1,1,256]{3,2,1,0:T(2,128)(2,1)} %bitcast.50, bf16[]{:T(256)} %broadcast.103), dimensions={1,2}, to_apply=%bitcast.46.reduce_sub_computation | reduce | bytes 14680066
  96.0 9.0 reshape.130
  105.1 5.2 all-to-all-start
  111.4 0.8 copy-done.2
  113.1 0.8 reshape.121
  113.9 14.1 broadcast_multiply_fusion
  128.0 24.3 %mul.98 = f32[28,64,32,64]{3,2,1,0:T(8,128)} reshape(f32[1,1,1792,2048]{3,2,1,0:T(8,128)} %broadcast_multiply_fusion) | data formatting | bytes 29360128 | tf_op jit(solution)/shard_map/mul | solution.py:42
  152.5 40.9 %all-to-all-done = bf16[8,2,229376]{2,1,0:T(2,128)(2,1)} async-done(((bf16[8,2,229376]{2,1,0:T(2,128)(2,1)}), bf16[8,2,229376]{2,1,0:T(2,128)(2,1)}, u32[]{:S(2)}, u32[]{:S(2)}) %all-to-all-start) | async-done | bytes 7340064 | tf_op jit(solution)/shard_map/all_to_all | solution.py:39
  193.4 12.1 reshape.131
  205.5 15.9 copy.46
  221.4 21.6 %reshape.112 = f32[28,64,32,64]{3,2,1,0:T(8,128)} reshape(f32[1,1,1792,8,256]{4,3,2,1,0:T(8,128)} %bitcast.47) | data formatting | bytes 29360128 | tf_op jit(solution)/shard_map/convert_element_type | solution.py:44
  243.1 29.9 %add.64 = f32[28,64,32,64]{3,2,1,0:T(8,128)} add(f32[28,64,32,64]{3,2,1,0:T(8,128)} %mul.98, f32[28,64,32,64]{3,2,1,0:T(8,128)} %reshape.112) | non-fusion elementwise | flops 3670016 | bytes 44040192 | tf_op jit(solution)/shard_map/add | solution.py:42
  273.0 52.6 %fusion = f32[28,32,64,64]{2,3,1,0:T(8,128)} fusion(f32[28,64,32,64]{3,2,1,0:T(8,128)} %add.64, f32[64]{0:T(128)S(1)} %get-tuple-element.5, f32[64]{0:T(128)S(1)} %get-tuple-element.4), kind=kOutput, calls=%fused_computation.2 | convolution fusion | flops 2818584576 | bytes 29360640 | tf_op jit(solution)/shard_map/ui,piqj,vj->pquv/dot_general | solution.py:20
  325.6 29.6 %fusion.7 = f32[28,32,64,64]{3,2,1,0:T(8,128)} fusion(f32[28,32,64,64]{2,3,1,0:T(8,128)} %fusion, f32[64]{0:T(128)S(1)} %get-tuple-element.5, f32[64]{0:T(128)S(1)} %get-tuple-element.4), kind=kOutput, calls=%fused_computation.21 | convolution fusion | flops 2818584576 | bytes 29360640 | tf_op jit(solution)/shard_map/ui,piqj,vj->pquv/dot_general | solution.py:20
  355.3 24.7 %reshape.101 = f32[28,32,4096]{2,1,0:T(8,128)} reshape(f32[28,32,64,64]{3,2,1,0:T(8,128)} %fusion.7) | data formatting | bytes 29360128 | tf_op jit(solution)/shard_map/reshape | solution.py:48
  380.0 398.1 %gather_fusion = f32[28672]{0:T(1024)S(1)} fusion(f32[28,32,4096]{2,1,0:T(8,128)} %reshape.101, s32[28672]{0:T(1024)S(1)} %reshape.115), kind=kCustom, calls=%fused_computation | custom fusion | bytes 573440 | tf_op jit(solution)/shard_map/jit(take_along_axis)/gather | solution.py:50
  778.6 156.3 %scatter_custom_fusion = f32[3670016]{0:T(1024)} fusion(s32[28672]{0:T(1024)} %reshape.121, f32[28672]{0:T(1024)S(1)} %reshape.123, f32[]{:T(128)} %constant.15.clone.1), kind=kCustom, calls=%fused_computation.7 | custom fusion | flops 28672 | bytes 14680576
  934.9 22.2 %reshape.102 = f32[28,32,64,64]{3,2,1,0:T(8,128)} reshape(f32[3670016]{0:T(1024)} %scatter_custom_fusion) | data formatting | bytes 29360128 | tf_op jit(solution)/shard_map/reshape | solution.py:51
  957.1 34.3 %fusion.5 = f32[28,32,64,64]{2,3,1,0:T(8,128)} fusion(f32[28,32,64,64]{3,2,1,0:T(8,128)} %reshape.102, f32[64]{0:T(128)S(1)} %copy-done.7, f32[64]{0:T(128)S(1)} %copy-done.5), kind=kOutput, calls=%fused_computation.19 | convolution fusion | flops 2818584576 | bytes 29360640 | tf_op jit(solution)/shard_map/ui,pquv,vj->piqj/dot_general | solution.py:24
  991.3 29.2 %convolution_bitcast_fusion = f32[28,64,32,64]{3,1,2,0:T(8,128)S(1)} fusion(f32[28,32,64,64]{2,3,1,0:T(8,128)} %fusion.5, f32[64]{0:T(128)S(1)} %copy-done.7, f32[64]{0:T(128)S(1)} %copy-done.5), kind=kOutput, calls=%fused_computation.6 | convolution fusion | flops 2818584576 | bytes 29360640 | tf_op jit(solution)/shard_map/ui,pquv,vj->piqj/dot_general | solution.py:24
  1020.6 19.3 %copy.33 = f32[28,64,32,64]{3,2,1,0:T(8,128)} copy(f32[28,64,32,64]{3,1,2,0:T(8,128)S(1)} %convolution_bitcast_fusion) | data formatting | bytes 29360128 | tf_op jit(solution)/shard_map/ui,pquv,vj->piqj/transpose | solution.py:24
  1039.9 25.4 %broadcast_in_dim.39 = f32[1,1792,2048]{2,1,0:T(8,128)} reshape(f32[28,64,32,64]{3,2,1,0:T(8,128)} %copy.33) | data formatting | bytes 29360128 | tf_op jit(solution)/shard_map/broadcast_in_dim | solution.py:55
  1065.3 494.5 %all-reduce.2.cloned.1.call-done = f32[1,1792,2048]{2,1,0:T(8,128)} async-done(((f32[1,1792,2048]{2,1,0:T(8,128)}), f32[1,1792,2048]{2,1,0:T(8,128)}) %all-reduce.2.cloned.1.call-update) | async-done | bytes 14680080 | tf_op jit(solution)/shard_map/psum | solution.py:54
  1559.7 32.1 %copy.35 = f32[1,1792,2048]{1,0,2:T(1,128)} copy(f32[1,1792,2048]{2,1,0:T(8,128)} %all-reduce.2.cloned.1.call-done) | data formatting | bytes 29360128 | tf_op jit(solution)/shard_map/psum | solution.py:54
  1591.8 5.6 all-to-all-start.1
  1597.4 25.4 %reshape.103 = f32[1,1,1792,2048]{3,2,1,0:T(8,128)} reshape(f32[28,64,32,64]{3,2,1,0:T(8,128)} %copy.33) | data formatting | bytes 29360128 | tf_op jit(solution)/shard_map/reshape | solution.py:52
  1622.8 15.8 reshape.111
  1638.6 20.9 %add_subtract_fusion = f32[1,1,1792,2048]{3,2,1,0:T(8,128)} fusion(f32[1,1,1792,2048]{3,2,1,0:T(8,128)} %reshape.103, f32[1,1,1792,2048]{3,2,1,0:T(8,128)} %reshape.111, f32[1,1,1792,2048]{3,2,1,0:T(8,128)} %param.4), kind=kLoop, calls=%fused_computation.5 | loop fusion | flops 11010048 | bytes 58720256 | tf_op jit(solution)/shard_map/sub | solution.py:53
  1659.6 99.3 %all-to-all-done.1 = f32[1,1792,2048]{1,0,2:T(1,128)} async-done(((f32[1,1792,2048]{1,0,2:T(1,128)}), f32[1,1792,2048]{1,0,2:T(1,128)}, u32[]{:S(2)}, u32[]{:S(2)}) %all-to-all-start.1) | async-done | bytes 14680096 | tf_op jit(solution)/shard_map/all_to_all | solution.py:55
  1758.9 11.3 copy.41
  1770.2 14.4 copy.36
  (34 shorter events, 3.1 us)
Async XLA Ops:
  7.2 103.7 %copy-start = (s32[28,32,4,32]{3,2,1,0:T(4,128)S(1)}, s32[28,32,4,32]{3,2,1,0:T(4,128)}, u32[]{:S(2)}) copy-start(s32[28,32,4,32]{3,2,1,0:T(4,128)} %param.5) | copy-start | bytes 1376260
  96.0 16.4 copy-start.9
  96.0 16.6 copy-start.8
  105.1 88.4 %all-to-all-start = ((bf16[8,2,229376]{2,1,0:T(2,128)(2,1)}), bf16[8,2,229376]{2,1,0:T(2,128)(2,1)}, u32[]{:S(2)}, u32[]{:S(2)}) async-start(bf16[8,2,229376]{2,1,0:T(2,128)(2,1)} %reshape.130), calls=%async_computation | async-start | bytes 14680064 | tf_op jit(solution)/shard_map/all_to_all | solution.py:39
  110.3 1449.5 %all-reduce.2.cloned.1.call-start = ((), (), s32[]{:S(2)}) async-start(), calls=%async_computation.2 | async-start | bytes 29360128 | tf_op jit(solution)/shard_map/psum | solution.py:54
  111.3 0.8 copy-start.2
  152.5 173.1 %copy-start.4 = (f32[64]{0:T(128)}, f32[64]{0:T(128)S(1)}, u32[]{:S(2)}) copy-start(f32[64]{0:T(128)S(1)} %get-tuple-element.4) | copy-start | bytes 772
  152.5 173.1 %copy-start.6 = (f32[64]{0:T(128)}, f32[64]{0:T(128)S(1)}, u32[]{:S(2)}) copy-start(f32[64]{0:T(128)S(1)} %get-tuple-element.5) | copy-start | bytes 772
  380.0 398.3 %copy-start.3 = (s32[28,32,1,32]{3,2,1,0:T(1,128)S(1)}, s32[28,32,1,32]{3,2,1,0:T(1,128)}, u32[]{:S(2)}) copy-start(s32[28,32,1,32]{3,2,1,0:T(1,128)} %copy-done.2) | copy-start | bytes 344068
  934.9 22.2 %copy-start.5 = (f32[64]{0:T(128)S(1)}, f32[64]{0:T(128)}, u32[]{:S(2)}) copy-start(f32[64]{0:T(128)} %copy-done.4) | copy-start | bytes 772
  934.9 22.2 %copy-start.7 = (f32[64]{0:T(128)S(1)}, f32[64]{0:T(128)}, u32[]{:S(2)}) copy-start(f32[64]{0:T(128)} %copy-done.6) | copy-start | bytes 772
  1591.8 167.0 %all-to-all-start.1 = ((f32[1,1792,2048]{1,0,2:T(1,128)}), f32[1,1792,2048]{1,0,2:T(1,128)}, u32[]{:S(2)}, u32[]{:S(2)}) async-start(f32[1,1792,2048]{1,0,2:T(1,128)} %copy.35), calls=%async_computation.1 | async-start | bytes 29360128 | tf_op jit(solution)/shard_map/all_to_all | solution.py:55
  1770.2 14.4 copy-start.1
Sparse Core Ops, SparseCore 0:
  1065.4 494.3 all-reduce.1
where the time goes:
time: 1810 us; the launch traced here: 1790 us
  local copies, waits for them, and re-layouts  689 us (38%)
  waiting for transfers between devices  635 us (35%)
  other arithmetic  297 us (16%)
  matrix products  146 us (8%)
    psum x1, waiting for transfers between devices, on_device(): total = lax.psum(restored, 'dp')  494 us
    gather x2, local copies, waits for them, and re-layouts, on_device(): values = jnp.take_along_axis(coeffs, own, axis=2)  398 us
    unnamed x5, other arithmetic  231 us
    all_to_all x1, waiting for transfers between devices, on_device(): lax.all_to_all(total[None], 'expert', split_axis=2, concat_axis=1, tiled=...  99.3 us
    dot_general x2, matrix products, forward(): jnp.einsum('ui,piqj,vj->pquv', cosine, blocks, cosine, precision=HIGHEST_...  82.3 us
    dot_general x2, matrix products, inverse(): jnp.einsum('ui,pquv,vj->piqj', cosine, coeffs, cosine, precision=HIGHEST_...  63.5 us
    convert_element_type x3, local copies, waits for them, and re-layouts, on_device(): decayed = MOMENTUM_DECAY * momentum.reshape(row_count, col_count) + shift...  53.4 us
    unnamed x26, local copies, waits for them, and re-layouts  48.5 us
  transfers between devices with their start and end apart: 3, of which 3 were waited for; matrix products, arithmetic and copies ran while one was open for 6% of the time, Pallas kernels for 0%

commit v1 on v0

--- a/solution.py
+++ b/solution.py
@@ -51,7 +51,7 @@
     selected = place(values, own, SPAN * SPAN).reshape(block_rows, block_cols, SPAN, SPAN)
     restored = inverse(selected, cosine).reshape(row_count, col_count)
     momentum_next = (decayed - restored).reshape(momentum.shape)
-    total = lax.psum(restored, "dp")
+    total = jnp.sum(lax.all_gather(restored, "dp"), axis=0)
     update = lax.all_to_all(total[None], "expert", split_axis=2, concat_axis=1, tiled=True)
     return (momentum_next, update)
 

time: 1810 us -> 2320 us (1.28)
  waiting for transfers between devices: 635 us -> 1120 us
  other arithmetic: 297 us -> 321 us
    all_gather x0 -> x1, waiting for transfers between devices: none -> 975 us  [on_device(): total = jnp.sum(lax.all_gather(restored, 'dp'), axis=0)]
    psum x1 -> x0, waiting for transfers between devices: 494 us -> none  [on_device(): total = lax.psum(restored, 'dp')]
    psum x1 -> x0, local copies, waits for them, and re-layouts: 32.1 us -> none  [on_device(): total = lax.psum(restored, 'dp')]
    another operation x0 -> x1, local copies, waits for them, and re-layouts: none -> 25.4 us  [on_device(): total = jnp.sum(lax.all_gather(restored, 'dp'), axis=0)]
    reduce_sum x0 -> x1, other arithmetic: none -> 24.8 us  [on_device(): total = jnp.sum(lax.all_gather(restored, 'dp'), axis=0)]
  transfers between devices with their start and end apart: 3 -> 3, of which waited for: 3 -> 3; matrix products, arithmetic and copies ran while one was open for 6% -> 4% of each run, Pallas kernels for 0% -> 0%
where the time goes in v1:
time: 2320 us; the launch traced here: 2300 us
  waiting for transfers between devices  1120 us (48%)
  local copies, waits for them, and re-layouts  689 us (30%)
  other arithmetic  321 us (14%)
  matrix products  146 us (6%)
    all_gather x1, waiting for transfers between devices, on_device(): total = jnp.sum(lax.all_gather(restored, 'dp'), axis=0)  975 us
    gather x2, local copies, waits for them, and re-layouts, on_device(): values = jnp.take_along_axis(coeffs, own, axis=2)  398 us
    unnamed x5, other arithmetic  231 us
    all_to_all x1, waiting for transfers between devices, on_device(): lax.all_to_all(total[None], 'expert', split_axis=2, concat_axis=1, tiled=...  99.3 us
    dot_general x2, matrix products, forward(): jnp.einsum('ui,piqj,vj->pquv', cosine, blocks, cosine, precision=HIGHEST_...  82.3 us
    dot_general x2, matrix products, inverse(): jnp.einsum('ui,pquv,vj->piqj', cosine, coeffs, cosine, precision=HIGHEST_...  63.5 us
    convert_element_type x3, local copies, waits for them, and re-layouts, on_device(): decayed = MOMENTUM_DECAY * momentum.reshape(row_count, col_count) + shift...  53.4 us
    unnamed x26, local copies, waits for them, and re-layouts  48.5 us
  transfers between devices with their start and end apart: 3, of which 3 were waited for; matrix products, arithmetic and copies ran while one was open for 4% of the time, Pallas kernels for 0%

profile of v1, /device:TPU:0, one launch (start us, length us, event | category | flops | bytes accessed | tf_op | source)
XLA Modules:
  0.0 2297.1 jit_solution(18206423486572765982)
XLA Ops:
  7.2 13.9 copy.44
  21.6 74.4 %reduce.4 = bf16[14336,256]{1,0:T(8,128)(2,1)} reduce(bf16[14336,1,1,256]{3,2,1,0:T(2,128)(2,1)} %bitcast.51, bf16[]{:T(256)} %broadcast.103), dimensions={1,2}, to_apply=%bitcast.47.reduce_sub_computation | reduce | bytes 14680066
  96.0 9.0 reshape.126
  105.1 5.2 all-to-all-start
  113.1 0.8 reshape.117
  113.9 14.1 broadcast_multiply_fusion
  128.0 24.3 %mul.98 = f32[28,64,32,64]{3,2,1,0:T(8,128)} reshape(f32[1,1,1792,2048]{3,2,1,0:T(8,128)} %broadcast_multiply_fusion) | data formatting | bytes 29360128 | tf_op jit(solution)/shard_map/mul | solution.py:42
  152.5 40.9 %all-to-all-done = bf16[8,2,229376]{2,1,0:T(2,128)(2,1)} async-done(((bf16[8,2,229376]{2,1,0:T(2,128)(2,1)}), bf16[8,2,229376]{2,1,0:T(2,128)(2,1)}, u32[]{:S(2)}, u32[]{:S(2)}) %all-to-all-start) | async-done | bytes 7340064 | tf_op jit(solution)/shard_map/all_to_all | solution.py:39
  193.4 12.1 reshape.127
  205.5 15.9 copy.43
  221.4 21.6 reshape.108
  243.1 29.9 %add.62 = f32[28,64,32,64]{3,2,1,0:T(8,128)} add(f32[28,64,32,64]{3,2,1,0:T(8,128)} %mul.98, f32[28,64,32,64]{3,2,1,0:T(8,128)} %reshape.108) | non-fusion elementwise | flops 3670016 | bytes 44040192 | tf_op jit(solution)/shard_map/add | solution.py:42
  273.0 52.6 %fusion = f32[28,32,64,64]{2,3,1,0:T(8,128)} fusion(f32[28,64,32,64]{3,2,1,0:T(8,128)} %add.62, f32[64]{0:T(128)S(1)} %get-tuple-element.5, f32[64]{0:T(128)S(1)} %get-tuple-element.4), kind=kOutput, calls=%fused_computation.2 | convolution fusion | flops 2818584576 | bytes 29360640 | tf_op jit(solution)/shard_map/ui,piqj,vj->pquv/dot_general | solution.py:20
  325.6 29.6 %fusion.7 = f32[28,32,64,64]{3,2,1,0:T(8,128)} fusion(f32[28,32,64,64]{2,3,1,0:T(8,128)} %fusion, f32[64]{0:T(128)S(1)} %get-tuple-element.5, f32[64]{0:T(128)S(1)} %get-tuple-element.4), kind=kOutput, calls=%fused_computation.21 | convolution fusion | flops 2818584576 | bytes 29360640 | tf_op jit(solution)/shard_map/ui,piqj,vj->pquv/dot_general | solution.py:20
  355.3 24.7 %reshape.99 = f32[28,32,4096]{2,1,0:T(8,128)} reshape(f32[28,32,64,64]{3,2,1,0:T(8,128)} %fusion.7) | data formatting | bytes 29360128 | tf_op jit(solution)/shard_map/reshape | solution.py:48
  380.0 398.3 %gather_fusion = f32[28672]{0:T(1024)S(1)} fusion(f32[28,32,4096]{2,1,0:T(8,128)} %reshape.99, s32[28672]{0:T(1024)S(1)} %reshape.111), kind=kCustom, calls=%fused_computation | custom fusion | bytes 573440 | tf_op jit(solution)/shard_map/jit(take_along_axis)/gather | solution.py:50
  778.8 156.3 %scatter_custom_fusion = f32[3670016]{0:T(1024)} fusion(s32[28672]{0:T(1024)} %reshape.117, f32[28672]{0:T(1024)S(1)} %reshape.119, f32[]{:T(128)} %constant.15.clone.1), kind=kCustom, calls=%fused_computation.7 | custom fusion | flops 28672 | bytes 14680576
  935.1 22.2 reshape.100
  957.3 34.3 %fusion.5 = f32[28,32,64,64]{2,3,1,0:T(8,128)} fusion(f32[28,32,64,64]{3,2,1,0:T(8,128)} %reshape.100, f32[64]{0:T(128)S(1)} %copy-done.7, f32[64]{0:T(128)S(1)} %copy-done.5), kind=kOutput, calls=%fused_computation.19 | convolution fusion | flops 2818584576 | bytes 29360640 | tf_op jit(solution)/shard_map/ui,pquv,vj->piqj/dot_general | solution.py:24
  991.5 29.2 %convolution_bitcast_fusion = f32[28,64,32,64]{3,1,2,0:T(8,128)S(1)} fusion(f32[28,32,64,64]{2,3,1,0:T(8,128)} %fusion.5, f32[64]{0:T(128)S(1)} %copy-done.7, f32[64]{0:T(128)S(1)} %copy-done.5), kind=kOutput, calls=%fused_computation.6 | convolution fusion | flops 2818584576 | bytes 29360640 | tf_op jit(solution)/shard_map/ui,pquv,vj->piqj/dot_general | solution.py:24
  1020.8 19.3 copy.30
  1040.1 25.4 %all_gather_reshape.3 = f32[1,1792,2048]{2,1,0:T(8,128)} reshape(f32[28,64,32,64]{3,2,1,0:T(8,128)} %copy.30) | data formatting | bytes 29360128 | tf_op jit(solution)/shard_map/all_gather;reshape | solution.py:54
  1065.5 975.1 %all-gather.2.cloned.1.call-done = f32[4,1792,2048]{2,1,0:T(8,128)} async-done(((f32[1,1792,2048]{2,1,0:T(8,128)}), f32[4,1792,2048]{2,1,0:T(8,128)}) %all-gather.2.cloned.1.call-update) | async-done | bytes 58720272 | tf_op jit(solution)/shard_map/all_gather | solution.py:54
  2040.5 24.8 %reduce_sum.9 = f32[1792,2048]{1,0:T(8,128)} reduce(f32[4,1792,2048]{2,1,0:T(8,128)} %all-gather.2.cloned.1.call-done, f32[]{:T(128)} %constant.15.clone.1), dimensions={0}, to_apply=%region_1.2 | reduce | flops 11010048 | bytes 73400320 | tf_op jit(solution)/shard_map/reduce_sum | solution.py:54
  2065.3 32.1 %copy.32 = f32[1,1792,2048]{1,0,2:T(1,128)} copy(f32[1,1792,2048]{2,1,0:T(8,128)} %bitcast.53) | data formatting | bytes 29360128 | tf_op jit(solution)/shard_map/broadcast_in_dim | solution.py:55
  2097.4 5.6 all-to-all-start.1
  2102.9 25.4 %reshape.101 = f32[1,1,1792,2048]{3,2,1,0:T(8,128)} reshape(f32[28,64,32,64]{3,2,1,0:T(8,128)} %copy.30) | data formatting | bytes 29360128 | tf_op jit(solution)/shard_map/reshape | solution.py:52
  2128.3 15.8 reshape.107
  2144.2 20.9 add_subtract_fusion
  2165.1 99.3 %all-to-all-done.1 = f32[1,1792,2048]{1,0,2:T(1,128)} async-done(((f32[1,1792,2048]{1,0,2:T(1,128)}), f32[1,1792,2048]{1,0,2:T(1,128)}, u32[]{:S(2)}, u32[]{:S(2)}) %all-to-all-start.1) | async-done | bytes 14680096 | tf_op jit(solution)/shard_map/all_to_all | solution.py:55
  2264.4 11.3 copy.38
  2275.7 14.4 copy.33
  (35 shorter events, 3.9 us)
Async XLA Ops:
  7.2 103.7 %copy-start = (s32[28,32,4,32]{3,2,1,0:T(4,128)S(1)}, s32[28,32,4,32]{3,2,1,0:T(4,128)}, u32[]{:S(2)}) copy-start(s32[28,32,4,32]{3,2,1,0:T(4,128)} %param.5) | copy-start | bytes 1376260
  96.0 16.4 copy-start.9
  96.0 16.6 copy-start.8
  105.1 88.4 %all-to-all-start = ((bf16[8,2,229376]{2,1,0:T(2,128)(2,1)}), bf16[8,2,229376]{2,1,0:T(2,128)(2,1)}, u32[]{:S(2)}, u32[]{:S(2)}) async-start(bf16[8,2,229376]{2,1,0:T(2,128)(2,1)} %reshape.126), calls=%async_computation | async-start | bytes 14680064 | tf_op jit(solution)/shard_map/all_to_all | solution.py:39
  110.3 1930.3 %all-gather.2.cloned.1.call-start = ((), (), s32[]{:S(2)}) async-start(), calls=%async_computation.2 | async-start | bytes 73400320 | tf_op jit(solution)/shard_map/all_gather | solution.py:54
  111.3 0.8 copy-start.2
  152.5 173.1 %copy-start.4 = (f32[64]{0:T(128)}, f32[64]{0:T(128)S(1)}, u32[]{:S(2)}) copy-start(f32[64]{0:T(128)S(1)} %get-tuple-element.4) | copy-start | bytes 772
  152.5 173.1 %copy-start.6 = (f32[64]{0:T(128)}, f32[64]{0:T(128)S(1)}, u32[]{:S(2)}) copy-start(f32[64]{0:T(128)S(1)} %get-tuple-element.5) | copy-start | bytes 772
  380.0 398.5 %copy-start.3 = (s32[28,32,1,32]{3,2,1,0:T(1,128)S(1)}, s32[28,32,1,32]{3,2,1,0:T(1,128)}, u32[]{:S(2)}) copy-start(s32[28,32,1,32]{3,2,1,0:T(1,128)} %copy-done.2) | copy-start | bytes 344068
  935.1 22.2 copy-start.5
  935.1 22.2 copy-start.7
  2097.4 167.0 %all-to-all-start.1 = ((f32[1,1792,2048]{1,0,2:T(1,128)}), f32[1,1792,2048]{1,0,2:T(1,128)}, u32[]{:S(2)}, u32[]{:S(2)}) async-start(f32[1,1792,2048]{1,0,2:T(1,128)} %copy.32), calls=%async_computation.1 | async-start | bytes 29360128 | tf_op jit(solution)/shard_map/all_to_all | solution.py:55
  2275.7 14.4 copy-start.1
Sparse Core Ops, SparseCore 0:
  1065.6 974.8 all-gather.1
